TPU v7x, 32 devices: a whole 2x2x4 slice. The times are simulated.
32 devices in a mesh: day: 8 (over y, x, core), pair: 4 (over z).
Axes of the slice: x: 2, y: 2, z: 4, core: 2. Of those that a mesh axis runs over, the one named last changes fastest.
Arguments:
- correlations: bfloat16 [32, 2048, 2001], P('day', 'pair'), may hold values from -8 to 8
- mask: int32 [32, 2048], P('day', 'pair'), may hold values from 0 to 1, as said below
- counts: int32 [2048], P(('pair', 'day')), may hold values from 1 to 32, as said below
Outputs:
- phase_weighted: float32 [2048, 2001], P(('pair', 'day'))
- linear: float32 [2048, 2001], P(('pair', 'day'))
Inputs may be any that keep to these rules, and one draw needn't show every extreme that they name: `mask`: every pair has a usable correlation on at least one day. counts[p] equals the number of days d with mask[d, p] = 1.
All inputs are finite; a program needn't handle non-finite values.
Results may differ from a plain program's by a relative error of at most 0.00044.
Values may be sent and summed in bfloat16 or wider, within the bound.
A program may use at most 128 MiB of HBM per device.

v0:
```python
import jax
import jax.numpy as jnp
from jax import lax
from jax.sharding import PartitionSpec as P


def hilbert_table(lag_count):
    row_index = lax.broadcasted_iota(jnp.int32, (lag_count, lag_count), 0)
    col_index = lax.broadcasted_iota(jnp.int32, (lag_count, lag_count), 1)
    offset = (col_index - row_index) % lag_count
    offset = jnp.where(offset > lag_count // 2, offset - lag_count, offset)
    phase_angle = jnp.pi * offset.astype(jnp.float32) / lag_count
    parity = 1.0 - 2.0 * (offset % 2).astype(jnp.float32)
    sine_safe = jnp.where(offset == 0, 1.0, jnp.sin(phase_angle))
    table = jnp.where(offset == 0, 0.0, (jnp.cos(phase_angle) - parity) / (lag_count * sine_safe))
    return table.astype(jnp.bfloat16)


def stack_terms(pieces, weight, kernel_table):
    day_count, pair_count, lag_count = pieces.shape
    flattened = pieces.reshape(day_count * pair_count, lag_count)
    hilbert = jnp.dot(flattened, kernel_table, preferred_element_type=jnp.float32)
    day_scale = weight[:, None, None]
    real_part = day_scale * pieces.astype(jnp.float32)
    imag_part = day_scale * hilbert.reshape(day_count, pair_count, lag_count)
    inverse = lax.rsqrt(real_part * real_part + imag_part * imag_part + 0.25)
    return (
        jnp.sum(real_part, axis=0),
        jnp.sum(real_part * inverse, axis=0),
        jnp.sum(imag_part * inverse, axis=0),
    )


def shards(correlations, mask, counts):
    masked = correlations * mask[:, :, None].astype(jnp.bfloat16)
    energy = jnp.sum(jnp.square(masked.astype(jnp.float32)), axis=(1, 2))
    used_pairs = jnp.sum(mask, axis=1).astype(jnp.float32)
    energy, used_pairs = lax.psum((energy, used_pairs), "pair")
    lag_count = correlations.shape[2]
    weight = lax.rsqrt(energy / (lag_count * jnp.maximum(used_pairs, 1.0)) + 0.1)
    kernel_table = hilbert_table(lag_count)
    groups = lax.axis_size("day")
    owned_rows = correlations.shape[1] // groups
    weights_all = lax.all_gather(weight, "day", axis=0, tiled=True)
    blocks = masked.reshape(correlations.shape[0], groups, owned_rows, lag_count)
    linear_sum, phase_real, phase_imag = stack_terms(
        lax.all_to_all(blocks, "day", split_axis=1, concat_axis=0, tiled=True)[:, 0],
        weights_all,
        kernel_table,
    )
    divisor = jnp.maximum(counts.astype(jnp.float32), 1.0)[:, None]
    linear = linear_sum / divisor
    coherence = (phase_real * phase_real + phase_imag * phase_imag) / (divisor * divisor)
    return (linear * coherence, linear)


def solution(mesh):
    placed = (P("day", "pair", None), P("day", "pair"), P(("pair", "day")))
    return jax.shard_map(
        shards,
        mesh=mesh,
        in_specs=placed,
        out_specs=(P(("pair", "day"), None), P(("pair", "day"), None)),
        check_vma=False,
    )
```

profile of v0, /device:TPU:0, one launch (start us, length us, event | category | flops | bytes accessed | tf_op | source)
XLA Modules:
  0.0 252.3 jit_solution(110081659509444308)
XLA Ops:
  0.6 0.9 fusion.38
  1.5 13.7 %copy.9 = bf16[4,512,2001]{2,1,0:T(8,128)(2,1)} copy(bf16[4,512,2001]{1,0,2:T(4,128)(2,1)} %param.3) | data formatting | bytes 16392192 | tf_op args[0]
  15.3 8.3 %multiply_reduce_fusion.3 = (f32[4]{0:T(128)S(1)}, bf16[4,512,2001]{2,1,0:T(8,128)(2,1)}) fusion(bf16[4,512,2001]{2,1,0:T(8,128)(2,1)} %copy.9, bf16[4,512]{1,0:T(4,128)(2,1)S(1)} %get-tuple-element.11), kind=kLoop, calls=%fused_computation.10 | loop fusion | flops 16392188 | bytes 16396304 | tf_op jit(solution)/shard_map/reduce_sum | solution.py:36
  23.6 8.3 %copy.10 = bf16[4,8,64,2001]{3,2,0,1:T(8,128)(2,1)} copy(bf16[4,8,64,2001]{3,2,1,0:T(8,128)(2,1)} %bitcast.22) | data formatting | bytes 16392192 | tf_op jit(solution)/shard_map/reshape | solution.py:45
  31.9 0.0 copy-start.1
  31.9 0.0 copy-start
  31.9 5.3 %all-to-all-start = ((bf16[4,8,64,2001]{3,2,0,1:T(8,128)(2,1)}), bf16[4,8,64,2001]{3,2,0,1:T(8,128)(2,1)}, u32[]{:S(2)}, u32[]{:S(2)}) async-start(bf16[4,8,64,2001]{3,2,0,1:T(8,128)(2,1)} %copy.10), calls=%async_computation | async-start | bytes 16777216 | tf_op jit(solution)/shard_map/all_to_all | solution.py:47
  37.2 13.2 %all-reduce.1 = (f32[4]{0:T(128)S(1)}, f32[4]{0:T(128)S(1)}) all-reduce(f32[4]{0:T(128)S(1)} %get-tuple-element.8, f32[4]{0:T(128)S(1)} %convert_element_type.30), channel_id=1, replica_groups=mesh['day'=8,'pair'=4] {'pair'}, use_global_device_ids=true, to_apply=%region_1.0 | all-reduce | flops 8 | bytes 64 | tf_op jit(solution)/shard_map/psum | solution.py:38
  50.4 0.0 copy-done.1
  50.4 0.6 dynamic-slice
  51.7 0.1 rsqrt_dynamic-update-slice_fusion
  51.8 85.9 %all-reduce = f32[32]{0:T(128)S(1)} all-reduce(f32[32]{0:T(128)S(1)} %rsqrt_dynamic-update-slice_fusion), channel_id=1, replica_groups=mesh['day'=8,'pair'=4] {'day'}, use_global_device_ids=true, to_apply=%add | all-reduce | flops 32 | bytes 256
  137.7 0.1 mul.71
  137.8 0.0 copy-done
  137.8 82.2 %fusion.14.clone.4 = bf16[2001,2001,1]{1,0,2:T(8,128)(2,1)} fusion(), kind=kLoop, calls=%fused_computation.24.clone.clone.clone.clone.1 | loop fusion | flops 132132008 | bytes 8008002 | tf_op jit(solution)/shard_map/reduce_sum | solution.py:29
  220.1 0.0 all-to-all-done
  220.1 0.0 copy-start.2
  220.1 5.9 %multiply_reduce_fusion.2 = f32[64,2001]{1,0:T(8,128)S(1)} fusion(bf16[4,8,64,2001]{3,2,0,1:T(8,128)(2,1)} %all-to-all-done, f32[8,4]{1,0:T(8,128)S(1)} %mul.71), kind=kLoop, calls=%fused_computation.9 | loop fusion | flops 12166080 | bytes 8708480 | tf_op jit(solution)/shard_map/reduce_sum | solution.py:28
  226.0 0.0 copy-done.2
  226.0 25.2 %multiply_reduce_fusion.1 = (f32[64,2001]{1,0:T(8,128)S(1)}, f32[64,2001]{1,0:T(8,128)S(1)}) fusion(f32[32]{0:T(128)S(1)} %all-reduce, bf16[4,8,64,2001]{3,2,0,1:T(8,128)(2,1)} %all-to-all-done, bf16[32,64,2001]{2,1,0:T(8,128)(2,1)} %bitcast.5, bf16[2001,2001,1]{1,0,2:T(8,128)(2,1)S(1)} %copy-done.2), kind=kOutput, calls=%fused_computation.6 | convolution fusion | flops 16445210624 | bytes 25424834 | tf_op jit(solution)/shard_map/dot_general | solution.py:22
  251.2 1.1 divide_multiply_fusion
  (3 shorter events, 0.0 us)
Async XLA Ops:
  31.9 18.6 %copy-start.1 = (u32[32]{0:T(128)S(1)}, u32[32]{0:T(128)}, u32[]{:S(2)}) copy-start(u32[32]{0:T(128)} %constant.54) | copy-start | bytes 388
  31.9 105.9 %copy-start = (s32[64]{0:T(128)S(1)}, s32[64]{0:T(128)}, u32[]{:S(2)}) copy-start(s32[64]{0:T(128)} %param.5) | copy-start | bytes 772
  31.9 188.2 %all-to-all-start = ((bf16[4,8,64,2001]{3,2,0,1:T(8,128)(2,1)}), bf16[4,8,64,2001]{3,2,0,1:T(8,128)(2,1)}, u32[]{:S(2)}, u32[]{:S(2)}) async-start(bf16[4,8,64,2001]{3,2,0,1:T(8,128)(2,1)} %copy.10), calls=%async_computation | async-start | bytes 16777216 | tf_op jit(solution)/shard_map/all_to_all | solution.py:47
  220.1 6.0 %copy-start.2 = (bf16[2001,2001,1]{1,0,2:T(8,128)(2,1)S(1)}, bf16[2001,2001,1]{1,0,2:T(8,128)(2,1)}, u32[]{:S(2)}) copy-start(bf16[2001,2001,1]{1,0,2:T(8,128)(2,1)} %fusion.14.clone.4) | copy-start | bytes 24024010
where the time goes:
time: 253 us; the launch traced here: 252 us
  blocking collectives  99.2 us (39%)
  other arithmetic  98.7 us (39%)
  matrix products  25.2 us (10%)
  local copies, waits for them, and re-layouts  22.7 us (9%)
  starting transfers between devices  5.33 us (2%)
    unnamed x1, blocking collectives  85.9 us
    reduce_sum x1, other arithmetic, stack_terms(): jnp.sum(real_part * inverse, axis=0)  82.2 us
    dot_general x1, matrix products, stack_terms(): jnp.dot(flattened, kernel_table, preferred_element_type=jnp.float32)  25.2 us
    unnamed x9, local copies, waits for them, and re-layouts  14.3 us
    psum x1, blocking collectives, shards(): energy, used_pairs = lax.psum((energy, used_pairs), 'pair')  13.2 us
    reduce_sum x1, other arithmetic, shards(): energy = jnp.sum(jnp.square(masked.astype(jnp.float32)), axis=(1, 2))  8.34 us
    reshape x1, local copies, waits for them, and re-layouts, shards(): masked.reshape(correlations.shape[0], groups, owned_rows, lag_count)  8.25 us
    reduce_sum x1, other arithmetic, stack_terms(): jnp.sum(real_part, axis=0)  5.95 us
  transfers between devices with their start and end apart: 1, of which 0 were waited for; matrix products, arithmetic and copies ran while one was open for 33% of the time, Pallas kernels for 0%

commit v1 on v0

v1 whole, which is shorter than its diff:
```python
import functools

import jax
import jax.numpy as jnp
import numpy as np
from jax import lax
from jax.experimental import pallas as pl
from jax.experimental.pallas import tpu as pltpu
from jax.sharding import PartitionSpec as P

TILE = 256
FULL = 32767.0
UNIT = 2.0**20


def padded(lag_count):
    return -(-lag_count // TILE) * TILE


def kernel_strip(lag_count):
    f32 = np.float32
    offset = np.arange(lag_count, dtype=np.int32)
    offset = np.where(offset > lag_count // 2, offset - lag_count, offset)
    angle = f32(np.pi) * offset.astype(f32) / f32(lag_count)
    parity = f32(1) - f32(2) * (offset % 2).astype(f32)
    sine = np.where(offset == 0, f32(1), np.sin(angle)).astype(f32)
    kernel = np.where(offset == 0, f32(0), (np.cos(angle) - parity) / (f32(lag_count) * sine))
    width = padded(lag_count)
    index = np.arange(2 * width - TILE)[None, :] - np.arange(TILE)[:, None] - (width - TILE)
    return kernel.astype(f32)[index % lag_count].astype(jnp.bfloat16)


def codes(values):
    top = jnp.max(jnp.abs(values), axis=1, keepdims=True)
    units = (top * UNIT).astype(jnp.int32) + 1
    step = FULL * UNIT / units.astype(jnp.float32)
    return jnp.round(values * step).astype(jnp.int32), units


def join(high, low):
    return high * 65536 + (low & 65535)


def split(word):
    low = ((word & 65535) ^ 32768) - 32768
    return word >> 16, low


def stack_kernel(lag_count, mine_ref, other_ref, scale_ref, strip_ref, out_ref, table, rows_ref, sums):
    width = table.shape[1]
    days, rows = mine_ref.shape[0], mine_ref.shape[1]
    total = 2 * days * rows
    last = width - TILE

    @pl.when(pl.program_id(0) == 0)
    def _():
        for i in range(width // TILE):
            start = width - TILE - i * TILE
            table[pl.ds(i * TILE, TILE), :] = strip_ref[:, start : start + width]
        col = lax.broadcasted_iota(jnp.int32, (width, TILE), 1) + last
        table[:, last:] = jnp.where(col < lag_count, table[:, last:], jnp.zeros_like(table[:, last:]))

    lane = lax.broadcasted_iota(jnp.int32, (days * rows, TILE), 1) + last
    for part, ref in enumerate((mine_ref, other_ref)):
        there = pl.ds(part * days * rows, days * rows)
        rows_ref[there, :last] = ref[:, :, :last].reshape(days * rows, last)
        tail = ref[:, :, last:].reshape(days * rows, TILE)
        rows_ref[there, last:] = jnp.where(lane < lag_count, tail, jnp.zeros_like(tail))

    scale = scale_ref[...].reshape(total, 1)
    for j in range(width // TILE):
        cols = slice(j * TILE, (j + 1) * TILE)
        hilbert = jnp.dot(rows_ref[...], table[:, cols], preferred_element_type=jnp.float32)
        real = scale * rows_ref[:, cols].astype(jnp.float32)
        imag = scale * hilbert
        inverse = lax.rsqrt(real * real + imag * imag + 0.25)
        for k, term in enumerate((real, real * inverse, imag * inverse)):
            sums[k, :, cols] = jnp.sum(term.reshape(2 * days, rows, TILE), axis=0)
    half = width // 2
    linear, linear_units = codes(sums[0])
    first, first_units = codes(sums[1])
    second, second_units = codes(sums[2])
    out_ref[0, :, :width] = join(first, second)
    out_ref[0, :, width : width + half] = join(linear[:, :half], linear[:, half:])
    pick = lax.broadcasted_iota(jnp.int32, (rows, 128), 1)
    out_ref[0, :, width + half :] = jnp.where(
        pick == 0, linear_units, jnp.where(pick == 1, first_units, second_units)
    )


def finish_kernel(lag_count, words_ref, counts_ref, weighted_ref, linear_ref):
    parts, rows, size = words_ref.shape
    width = (size - 128) * 2 // 3
    half = width // 2
    linear = real = imag = 0.0
    for k in range(parts):
        units = words_ref[k, :, width + half :].astype(jnp.float32) * (1.0 / (FULL * UNIT))
        first, second = split(words_ref[k, :, :width])
        left, right = split(words_ref[k, :, width : width + half])
        both = jnp.concatenate([left, right], axis=1)
        linear += both.astype(jnp.float32) * units[:, 0:1]
        real += first.astype(jnp.float32) * units[:, 1:2]
        imag += second.astype(jnp.float32) * units[:, 2:3]
    inverse = 1.0 / jnp.maximum(counts_ref[...].astype(jnp.float32), 1.0)
    linear = linear * inverse
    weighted = linear * ((real * real + imag * imag) * (inverse * inverse))
    linear_ref[...] = linear[:, :lag_count]
    weighted_ref[...] = weighted[:, :lag_count]


def shards(correlations, mask, counts):
    days, pairs, lag_count = correlations.shape
    groups = lax.axis_size("day")
    me = lax.axis_index("day")
    core = me % 2
    owned = pairs // groups
    width = padded(lag_count)

    squares = jnp.sum(jnp.square(correlations.astype(jnp.float32)), axis=2)
    mask_f = mask.astype(jnp.float32)
    local = jnp.stack([jnp.sum(squares * mask_f, axis=1), jnp.sum(mask_f, axis=1)])
    slots = lax.dynamic_update_slice(jnp.zeros((2, groups * days), jnp.float32), local, (0, me * days))
    energy, used = lax.psum(slots, ("day", "pair"))
    weight = lax.rsqrt(energy / (lag_count * jnp.maximum(used, 1.0)) + 0.1)

    couple = [(i, i ^ 1) for i in range(groups)]
    blocks = correlations.reshape(days, groups // 2, 2, owned, lag_count)
    mask_blocks = mask_f.reshape(days, groups // 2, 2, owned)
    mine, other = (jnp.where(core == 0, blocks[:, :, s], blocks[:, :, 1 - s]) for s in (0, 1))
    mask_mine, mask_other = (jnp.where(core == 0, mask_blocks[:, :, s], mask_blocks[:, :, 1 - s]) for s in (0, 1))
    other = lax.ppermute(other, "day", couple)
    mask_other = lax.ppermute(mask_other, "day", couple)

    weight_mine = lax.dynamic_slice(weight, (me * days,), (days,))
    weight_other = lax.dynamic_slice(weight, ((me ^ 1) * days,), (days,))
    scale = jnp.concatenate(
        [mask_mine * weight_mine[:, None, None], mask_other * weight_other[:, None, None]], axis=0
    )[..., None]

    strip = jnp.asarray(kernel_strip(lag_count))
    size = width + width // 2 + 128
    words = pl.pallas_call(
        functools.partial(stack_kernel, lag_count),
        grid=(groups // 2,),
        in_specs=[
            pl.BlockSpec((days, None, owned, width), lambda g: (0, g, 0, 0)),
            pl.BlockSpec((days, None, owned, width), lambda g: (0, g, 0, 0)),
            pl.BlockSpec((2 * days, None, owned, 1), lambda g: (0, g, 0, 0)),
            pl.BlockSpec(strip.shape, lambda g: (0, 0)),
        ],
        out_specs=pl.BlockSpec((1, owned, size), lambda g: (g, 0, 0)),
        out_shape=jax.ShapeDtypeStruct((groups // 2, owned, size), jnp.int32),
        scratch_shapes=[
            pltpu.VMEM((width, width), jnp.bfloat16),
            pltpu.VMEM((2 * days * owned, width), jnp.bfloat16),
            pltpu.VMEM((3, owned, width), jnp.float32),
        ],
        compiler_params=pltpu.CompilerParams(vmem_limit_bytes=60 * 2**20),
        cost_estimate=pl.CostEstimate(
            flops=2 * days * pairs * width * width, bytes_accessed=days * pairs * width * 2, transcendentals=0
        ),
        name="stack",
    )(mine, other, scale, strip)

    same = [[c + 2 * i for i in range(groups // 2)] for c in range(2)]
    words = lax.all_to_all(words, "day", split_axis=0, concat_axis=0, axis_index_groups=same, tiled=True)

    out = jax.ShapeDtypeStruct((owned, lag_count), jnp.float32)
    return pl.pallas_call(
        functools.partial(finish_kernel, lag_count),
        out_shape=(out, out),
        compiler_params=pltpu.CompilerParams(vmem_limit_bytes=60 * 2**20),
        name="finish",
    )(words, counts[:, None])


def solution(mesh):
    placed = (P("day", "pair", None), P("day", "pair"), P(("pair", "day")))
    return jax.shard_map(
        shards,
        mesh=mesh,
        in_specs=placed,
        out_specs=(P(("pair", "day"), None), P(("pair", "day"), None)),
        check_vma=False,
    )
```

time: 253 us -> 150 us (0.59)
  other arithmetic: 98.7 us -> 16.3 us
  blocking collectives: 99.2 us -> 42.1 us
  waiting for transfers between devices: 0.01 us -> 36.2 us
  Pallas kernels: 0 us -> 31.2 us
  matrix products: 25.2 us -> 0 us
  local copies, waits for them, and re-layouts: 22.7 us -> 17.9 us
    reduce_sum x4 -> x2, other arithmetic: 97.4 us -> 10.4 us  [the longest x1 10.3 us: shards(): squares = jnp.sum(jnp.square(correlations.astype(jnp.float32)), axis=2)]
    unnamed x1 -> x0, blocking collectives: 85.9 us -> none
    all_to_all x1, waiting for transfers between devices: 0.01 us -> 36.2 us  [shards(): lax.all_to_all(words, 'day', split_axis=0, concat_axis=0, axis_index_grou...]
    pallas_call x0 -> x2, Pallas kernels: none -> 31.2 us  [the longest x1 27.2 us: shards(): pl.pallas_call(functools.partial(stack_kernel, lag_count), grid=(groups /...]
    psum x1, blocking collectives: 13.2 us -> 42.1 us  [shards(): energy, used = lax.psum(slots, ('day', 'pair'))]
    dot_general x1 -> x0, matrix products: 25.2 us -> none  [stack_terms(): jnp.dot(flattened, kernel_table, preferred_element_type=jnp.float32)]
    reshape x1, local copies, waits for them, and re-layouts: 8.25 us -> 0.09 us  [shards(): mask_blocks = mask_f.reshape(days, groups // 2, 2, owned)]
    select_n x0 -> x1, other arithmetic: none -> 5.69 us  [shards(): jnp.where(core == 0, blocks[:, :, s], blocks[:, :, 1 - s])]
  transfers between devices with their start and end apart: 1 -> 3, of which waited for: 0 -> 1; matrix products, arithmetic and copies ran while one was open for 33% -> 9% of each run, Pallas kernels for 0% -> 0%
where the time goes in v1:
time: 150 us; the launch traced here: 149 us
  blocking collectives  42.1 us (28%)
  waiting for transfers between devices  36.2 us (24%)
  Pallas kernels  31.2 us (21%)
  local copies, waits for them, and re-layouts  17.9 us (12%)
  other arithmetic  16.3 us (11%)
  starting transfers between devices  4.42 us (3%)
    psum x1, blocking collectives, shards(): energy, used = lax.psum(slots, ('day', 'pair'))  42.1 us
    all_to_all x1, waiting for transfers between devices, shards(): lax.all_to_all(words, 'day', split_axis=0, concat_axis=0, axis_index_grou...  36.2 us
    pallas_call x1, Pallas kernels, shards(): pl.pallas_call(functools.partial(stack_kernel, lag_count), grid=(groups /...  27.2 us
    unnamed x7, local copies, waits for them, and re-layouts  15.4 us
    reduce_sum x1, other arithmetic, shards(): squares = jnp.sum(jnp.square(correlations.astype(jnp.float32)), axis=2)  10.3 us
    select_n x1, other arithmetic, shards(): jnp.where(core == 0, blocks[:, :, s], blocks[:, :, 1 - s])  5.69 us
    pallas_call x1, Pallas kernels, shards(): pl.pallas_call(functools.partial(finish_kernel, lag_count), out_shape=(ou...  4.04 us
    all_to_all x1, starting transfers between devices, shards(): lax.all_to_all(words, 'day', split_axis=0, concat_axis=0, axis_index_grou...  3.84 us
  transfers between devices with their start and end apart: 3, of which 1 were waited for; matrix products, arithmetic and copies ran while one was open for 9% of the time, Pallas kernels for 0%

profile of v1, /device:TPU:0, one launch (start us, length us, event | category | flops | bytes accessed | tf_op | source)
XLA Modules:
  0.0 148.8 jit_solution(5669912633787224958)
XLA Ops:
  0.6 13.7 %copy.7 = bf16[4,512,2001]{2,1,0:T(8,128)(2,1)} copy(bf16[4,512,2001]{1,0,2:T(4,128)(2,1)} %param.4) | data formatting | bytes 16392192 | tf_op args[0]
  14.4 0.0 copy-start.1
  14.4 5.7 %select_bitcast_fusion = (bf16[4,4,64,2001]{3,2,1,0:T(8,128)(2,1)}, bf16[4,4,64,2001]{3,2,1,0:T(8,128)(2,1)}) fusion(pred[]{:T(512)S(6)} %eq.4, bf16[4,4,2,64,2001]{4,3,2,1,0:T(8,128)(2,1)} %bitcast.33), kind=kLoop, calls=%fused_computation.3 | loop fusion | flops 4098048 | bytes 16392193 | tf_op jit(solution)/shard_map/jit(_where)/select_n | solution.py:129
  20.1 0.5 collective-permute-start
  20.6 0.0 copy-done.1
  20.6 0.1 reshape.28
  20.7 0.1 collective-permute-start.1
  20.8 10.3 %multiply_reduce_fusion = f32[4,512]{1,0:T(4,128)S(1)} fusion(bf16[4,512,2001]{1,0,2:T(4,128)(2,1)} %param.4), kind=kLoop, calls=%fused_computation | loop fusion | flops 12292096 | bytes 8204288 | tf_op jit(solution)/shard_map/reduce_sum | solution.py:119
  31.1 0.1 multiply_reduce_fusion.1
  31.2 0.1 dynamic_update_slice.3
  31.4 42.1 %psum.7 = f32[2,32]{1,0:T(2,128)S(1)} all-reduce(f32[2,32]{1,0:T(2,128)S(1)} %dynamic_update_slice.3), channel_id=1, replica_groups=mesh['day'=8,'pair'=4] {'day','pair'}, use_global_device_ids=true, to_apply=%region_3.4 | all-reduce | flops 64 | bytes 512 | tf_op jit(solution)/shard_map/psum | solution.py:123
  73.5 0.1 dynamic-slice_bitcast_fusion.1
  73.5 0.1 bitcast_multiply_fusion
  73.6 0.0 collective-permute-done.1
  73.6 0.1 broadcast_multiply_fusion
  73.7 1.5 copy.15.scale_ref
  75.2 0.0 collective-permute-done.other_ref
  75.2 27.2 %stack.13 = s32[4,64,3200]{2,1,0:T(8,128)} custom-call(bf16[4,4,64,2001]{3,2,1,0:T(8,128)(2,1)} %get-tuple-element.5.mine_ref, bf16[4,4,64,2001]{3,2,1,0:T(8,128)(2,1)} %collective-permute-done.other_ref, f32[8,4,64,1]{3,2,1,0:T(8,128)} %copy.15.scale_ref, bf16[256,3840]{1,0:T(8,128)(2,1)} %constant.36.clone.strip_ref), custom_call_target="tpu_custom_call" | custom-call | flops 17179869184 | bytes 8388608 | tf_op jit(solution)/shard_map/stack/pallas_call | solution.py:142
  102.3 0.0 copy-start.2
  102.3 3.8 %all-to-all-start = ((s32[4,64,3200]{2,1,0:T(8,128)}), s32[4,64,3200]{2,1,0:T(8,128)S(1)}, u32[]{:S(2)}, u32[]{:S(2)}) async-start(s32[4,64,3200]{2,1,0:T(8,128)} %stack.13), calls=%async_computation | async-start | bytes 6553600 | tf_op jit(solution)/shard_map/all_to_all | solution.py:166
  106.2 0.0 copy-done.2
  106.2 0.7 copy.16.counts_ref
  106.9 36.2 %all-to-all-done.words_ref = s32[4,64,3200]{2,1,0:T(8,128)S(1)} async-done(((s32[4,64,3200]{2,1,0:T(8,128)}), s32[4,64,3200]{2,1,0:T(8,128)S(1)}, u32[]{:S(2)}, u32[]{:S(2)}) %all-to-all-start) | async-done | bytes 3276832 | tf_op jit(solution)/shard_map/all_to_all | solution.py:166
  143.1 0.0 copy-start
  143.1 1.7 %copy-done = s32[4,64,3200]{2,1,0:T(8,128)} copy-done((s32[4,64,3200]{2,1,0:T(8,128)}, s32[4,64,3200]{2,1,0:T(8,128)S(1)}, u32[]{:S(2)}) %copy-start) | copy-done | bytes 3276824
  144.8 4.0 %finish.1 = (f32[64,2001]{1,0:T(8,128)}, f32[64,2001]{1,0:T(8,128)}) custom-call(s32[4,64,3200]{2,1,0:T(8,128)} %copy-done, s32[64,1]{1,0:T(8,128)} %copy.16.counts_ref), custom_call_target="tpu_custom_call" | custom-call | tf_op jit(solution)/shard_map/finish/pallas_call | solution.py:169
  (6 shorter events, 0.1 us)
Async XLA Ops:
  14.4 6.2 %copy-start.1 = (s32[4,512]{1,0:T(4,128)S(1)}, s32[4,512]{1,0:T(4,128)}, u32[]{:S(2)}) copy-start(s32[4,512]{1,0:T(4,128)} %param.5) | copy-start | bytes 24580
  20.1 55.1 %collective-permute-start = (bf16[4,4,64,2001]{3,2,1,0:T(8,128)(2,1)}, bf16[4,4,64,2001]{3,2,1,0:T(8,128)(2,1)}, u32[]{:S(2)}, u32[]{:S(2)}) collective-permute-start(bf16[4,4,64,2001]{3,2,1,0:T(8,128)(2,1)} %get-tuple-element.4), channel_id=1, source_target_pairs={{0,4},{4,0},{8,12},{12,8},{16,20},{20,16},{24,28},{28,24},{1,5},{5... | collective-permute-start | bytes 12294152 | tf_op jit(solution)/shard_map/ppermute | solution.py:131
  20.7 52.9 %collective-permute-start.1 = (f32[4,4,64]{2,1,0:T(4,128)S(1)}, f32[4,4,64]{2,1,0:T(4,128)S(1)}, u32[]{:S(2)}, u32[]{:S(2)}) collective-permute-start(f32[4,4,64]{2,1,0:T(4,128)S(1)} %bitcast.36), channel_id=1, source_target_pairs={{0,4},{4,0},{8,12},{12,8},{16,20},{20,16},{24,28},{28,24},{1,5},{5... | collective-permute-start | bytes 12296 | tf_op jit(solution)/shard_map/ppermute | solution.py:132
  102.3 3.9 %copy-start.2 = (s32[64]{0:T(128)S(1)}, s32[64]{0:T(128)}, u32[]{:S(2)}) copy-start(s32[64]{0:T(128)} %param.6) | copy-start | bytes 772
  102.3 40.8 %all-to-all-start = ((s32[4,64,3200]{2,1,0:T(8,128)}), s32[4,64,3200]{2,1,0:T(8,128)S(1)}, u32[]{:S(2)}, u32[]{:S(2)}) async-start(s32[4,64,3200]{2,1,0:T(8,128)} %stack.13), calls=%async_computation | async-start | bytes 6553600 | tf_op jit(solution)/shard_map/all_to_all | solution.py:166
  143.1 1.7 %copy-start = (s32[4,64,3200]{2,1,0:T(8,128)}, s32[4,64,3200]{2,1,0:T(8,128)S(1)}, u32[]{:S(2)}) copy-start(s32[4,64,3200]{2,1,0:T(8,128)S(1)} %all-to-all-done.words_ref) | copy-start | bytes 9830404

commit v2 on v0

v2 whole, which is shorter than its diff:
```python
import functools

import jax
import jax.numpy as jnp
import numpy as np
from jax import lax
from jax.experimental import pallas as pl
from jax.experimental.pallas import tpu as pltpu
from jax.sharding import PartitionSpec as P

TILE = 256
MESH = pl.DeviceIdType.MESH
FULL = 32767.0
UNIT = 2.0**20


def padded(lag_count):
    return -(-lag_count // TILE) * TILE


def kernel_strip(lag_count):
    f32 = np.float32
    offset = np.arange(lag_count, dtype=np.int32)
    offset = np.where(offset > lag_count // 2, offset - lag_count, offset)
    angle = f32(np.pi) * offset.astype(f32) / f32(lag_count)
    parity = f32(1) - f32(2) * (offset % 2).astype(f32)
    sine = np.where(offset == 0, f32(1), np.sin(angle)).astype(f32)
    kernel = np.where(offset == 0, f32(0), (np.cos(angle) - parity) / (f32(lag_count) * sine))
    width = padded(lag_count)
    index = np.arange(2 * width - TILE)[None, :] - np.arange(TILE)[:, None] - (width - TILE)
    return kernel.astype(f32)[index % lag_count].astype(jnp.bfloat16)


def codes(values):
    top = jnp.max(jnp.abs(values), axis=1, keepdims=True)
    units = (top * UNIT).astype(jnp.int32) + 1
    step = FULL * UNIT / units.astype(jnp.float32)
    return jnp.round(values * step).astype(jnp.int32), units


def join(high, low):
    return high * 65536 + (low & 65535)


def split(word):
    low = ((word & 65535) ^ 32768) - 32768
    return word >> 16, low


def stack_kernel(
    lag_count, x_hbm, mask_ref, counts_ref, strip_hbm, weighted_ref, linear_ref,
    rows_ref, stage, strip, table, sums, day_weight, stat_out, stat_in, words_out, words_in,
    load_sem, stage_sem, strip_sem, swap_send, swap_recv, stat_send, stat_recv, word_send, word_recv,
):
    width = table.shape[1]
    half = width // 2
    chips, all_days, owned, _ = rows_ref.shape
    days = all_days // 2
    total = all_days * owned
    peers = stat_in.shape[0]
    me, plane = lax.axis_index("day"), lax.axis_index("pair")
    chip, core = me // 2, me % 2
    last = width - TILE

    def mine(g):
        return pltpu.make_async_copy(x_hbm.at[:, 2 * g + core], rows_ref.at[g, pl.ds(0, days)], load_sem.at[g])

    def staged(g):
        return pltpu.make_async_copy(x_hbm.at[:, 2 * g + 1 - core], stage.at[g], stage_sem.at[g])

    def swapped(g):
        return pltpu.make_async_remote_copy(
            stage.at[g], rows_ref.at[g, pl.ds(days, days)], swap_send.at[g], swap_recv.at[g],
            device_id={"day": me ^ 1, "pair": plane}, device_id_type=MESH,
        )

    def peer(o):
        rank = (2 * plane + core + o) % (peers + 1)
        return {"day": 2 * chip + rank % 2, "pair": rank // 2}

    def told(o):
        return pltpu.make_async_remote_copy(
            stat_out, stat_in.at[o - 1], stat_send.at[o - 1], stat_recv.at[o - 1],
            device_id=peer(o), device_id_type=MESH,
        )

    def owner(o):
        return {"day": 2 * (chip ^ o) + core, "pair": plane}

    def shipped(o):
        return pltpu.make_async_remote_copy(
            words_out.at[o - 1], words_in.at[o - 1], word_send.at[o - 1], word_recv.at[o - 1],
            device_id=owner(o), device_id_type=MESH,
        )

    for g in range(chips):
        staged(g).start()
    for g in range(chips):
        mine(g).start()
    strip_copy = pltpu.make_async_copy(strip_hbm, strip, strip_sem)
    strip_copy.start()

    barrier = pltpu.get_barrier_semaphore()
    for o in range(1, peers + 1):
        pl.semaphore_signal(barrier, inc=1, device_id=peer(o), device_id_type=MESH)
    for o in range(1, chips):
        pl.semaphore_signal(barrier, inc=1, device_id=owner(o), device_id_type=MESH)
    pl.semaphore_wait(barrier, peers + chips - 1)

    for g in range(chips):
        staged(g).wait()
        swapped(g).start()

    def statistics(g, carry):
        mine(g).wait()
        swapped(g).wait_recv()
        x = rows_ref[g].reshape(total, lag_count).astype(jnp.float32)
        row_mask = mask_ref[g]
        energy = jnp.sum(x * x, axis=1, keepdims=True) * row_mask
        both = jnp.concatenate(
            [jnp.broadcast_to(energy, (total, 128)), jnp.broadcast_to(row_mask, (total, 128))], axis=1
        )
        return carry + jnp.sum(both.reshape(all_days, owned, 256), axis=1)

    found = lax.fori_loop(0, chips, statistics, jnp.zeros((all_days, 256), jnp.float32))
    turned = jnp.concatenate([found[days:], found[:days]], axis=0)
    stat_out[...] = jnp.where(core == 0, found, turned)
    for o in range(1, peers + 1):
        told(o).start()

    strip_copy.wait()
    for i in range(width // TILE):
        start = width - TILE - i * TILE
        table[pl.ds(i * TILE, TILE), :] = strip[:, start : start + width]
    sums[:, :, last:] = jnp.zeros((3, owned, TILE), jnp.float32)

    for o in range(1, peers + 1):
        told(o).wait_recv()
    stats = stat_out[...]
    for o in range(peers):
        stats = stats + stat_in[o]
    weight = lax.rsqrt(stats[:, :128] / (lag_count * jnp.maximum(stats[:, 128:], 1.0)) + 0.1)
    weight = jnp.where(core == 0, weight, jnp.concatenate([weight[days:], weight[:days]], axis=0))
    for d in range(all_days):
        day_weight[pl.ds(d * owned, owned), :] = jnp.broadcast_to(weight[d : d + 1, :1], (owned, 1))

    def block(step, carry):
        o = chips - 1 - step
        g = chip ^ o
        scale = day_weight[...] * mask_ref[g]
        for j in range(width // TILE):
            cols = slice(j * TILE, min((j + 1) * TILE, lag_count))
            size = cols.stop - cols.start
            lhs = rows_ref[g].reshape(total, lag_count)
            hilbert = jnp.dot(lhs, table[:lag_count, cols], preferred_element_type=jnp.float32)
            real = scale * rows_ref[g, :, :, cols].reshape(total, size).astype(jnp.float32)
            imag = scale * hilbert
            inverse = lax.rsqrt(real * real + imag * imag + 0.25)
            for k, term in enumerate((real, real * inverse, imag * inverse)):
                sums[k, :, cols] = jnp.sum(term.reshape(all_days, owned, size), axis=0)

        @pl.when(o > 0)
        def _():
            linear, linear_units = codes(sums[0])
            first, first_units = codes(sums[1])
            second, second_units = codes(sums[2])
            words_out[o - 1, :, :width] = join(first, second)
            words_out[o - 1, :, width : width + half] = join(linear[:, :half], linear[:, half:])
            pick = lax.broadcasted_iota(jnp.int32, (owned, 128), 1)
            words_out[o - 1, :, width + half :] = jnp.where(
                pick == 0, linear_units, jnp.where(pick == 1, first_units, second_units)
            )
            shipped(o).start()

        return carry

    lax.fori_loop(0, chips, block, 0)

    def arrive(step, carry):
        o = chips - 1 - step
        shipped(o).wait_recv()
        units = words_in[o - 1, :, width + half :].astype(jnp.float32) * (1.0 / (FULL * UNIT))
        left, right = split(words_in[o - 1, :, width : width + half])
        sums[0, :, :half] += left.astype(jnp.float32) * units[:, 0:1]
        sums[0, :, half:] += right.astype(jnp.float32) * units[:, 0:1]
        first, second = split(words_in[o - 1, :, :width])
        sums[1] += first.astype(jnp.float32) * units[:, 1:2]
        sums[2] += second.astype(jnp.float32) * units[:, 2:3]
        return carry

    lax.fori_loop(0, chips - 1, arrive, 0)
    inverse = 1.0 / jnp.maximum(counts_ref[...].astype(jnp.float32), 1.0)
    linear = sums[0, :, :lag_count] * inverse
    real, imag = sums[1, :, :lag_count], sums[2, :, :lag_count]
    linear_ref[...] = linear
    weighted_ref[...] = linear * ((real * real + imag * imag) * (inverse * inverse))

    for g in range(chips):
        swapped(g).wait_send()
    for o in range(1, peers + 1):
        told(o).wait_send()
    for o in range(1, chips):
        shipped(o).wait_send()


def shards(correlations, mask, counts):
    days, pairs, lag_count = correlations.shape
    groups = lax.axis_size("day")
    chips = groups // 2
    core = lax.axis_index("day") % 2
    owned = pairs // groups
    width = padded(lag_count)
    peers = 2 * lax.axis_size("pair") - 1

    mask_blocks = mask.astype(jnp.float32).reshape(days, chips, 2, owned)
    mask_mine, mask_other = (jnp.where(core == 0, mask_blocks[:, :, s], mask_blocks[:, :, 1 - s]) for s in (0, 1))
    mask_other = lax.ppermute(mask_other, "day", [(i, i ^ 1) for i in range(groups)])
    row_mask = jnp.concatenate([mask_mine, mask_other], axis=0).transpose(1, 0, 2)
    row_mask = row_mask.reshape(chips, 2 * days * owned, 1)

    strip = jnp.asarray(kernel_strip(lag_count))
    size = width + width // 2 + 128
    out = jax.ShapeDtypeStruct((owned, lag_count), jnp.float32)
    vmem = pl.BlockSpec(memory_space=pltpu.VMEM)
    hbm = pl.BlockSpec(memory_space=pl.ANY)
    dma = pltpu.SemaphoreType.DMA
    return pl.pallas_call(
        functools.partial(stack_kernel, lag_count),
        in_specs=[hbm, vmem, vmem, hbm],
        out_specs=(vmem, vmem),
        out_shape=(out, out),
        scratch_shapes=[
            pltpu.VMEM((chips, 2 * days, owned, lag_count), jnp.bfloat16),
            pltpu.VMEM((chips, days, owned, lag_count), jnp.bfloat16),
            pltpu.VMEM(strip.shape, jnp.bfloat16),
            pltpu.VMEM((width, width), jnp.bfloat16),
            pltpu.VMEM((3, owned, width), jnp.float32),
            pltpu.VMEM((2 * days * owned, 1), jnp.float32),
            pltpu.VMEM((2 * days, 256), jnp.float32),
            pltpu.VMEM((peers, 2 * days, 256), jnp.float32),
            pltpu.VMEM((chips - 1, owned, size), jnp.int32),
            pltpu.VMEM((chips - 1, owned, size), jnp.int32),
            dma((chips,)), dma((chips,)), dma, dma((chips,)), dma((chips,)),
            dma((peers,)), dma((peers,)), dma((chips - 1,)), dma((chips - 1,)),
        ],
        compiler_params=pltpu.CompilerParams(
            vmem_limit_bytes=62 * 2**20, collective_id=0, has_side_effects=True
        ),
        name="stack",
    )(correlations.reshape(days, groups, owned, lag_count), row_mask, counts[:, None], strip)


def solution(mesh):
    placed = (P("day", "pair", None), P("day", "pair"), P(("pair", "day")))
    return jax.shard_map(
        shards,
        mesh=mesh,
        in_specs=placed,
        out_specs=(P(("pair", "day"), None), P(("pair", "day"), None)),
        check_vma=False,
    )
```

time: 253 us -> 86.7 us (0.34)
  blocking collectives: 99.2 us -> 0 us
  other arithmetic: 98.7 us -> 0.72 us
  Pallas kernels: 0 us -> 63.1 us
  matrix products: 25.2 us -> 0 us
  starting transfers between devices: 5.33 us -> 0.56 us
    reduce_sum x4 -> x0, other arithmetic: 97.4 us -> none  [the longest x1 82.2 us: stack_terms(): jnp.sum(real_part * inverse, axis=0)]
    unnamed x1 -> x0, blocking collectives: 85.9 us -> none
    pallas_call x0 -> x1, Pallas kernels: none -> 63.1 us  [shards(): pl.pallas_call(functools.partial(stack_kernel, lag_count), in_specs=[hbm,...]
    dot_general x1 -> x0, matrix products: 25.2 us -> none  [stack_terms(): jnp.dot(flattened, kernel_table, preferred_element_type=jnp.float32)]
    psum x1 -> x0, blocking collectives: 13.2 us -> none  [shards(): energy, used_pairs = lax.psum((energy, used_pairs), 'pair')]
    reshape x1 -> x2, local copies, waits for them, and re-layouts: 8.25 us -> 2.15 us  [the longest x1 2.06 us: shards(): row_mask = row_mask.reshape(chips, 2 * days * owned, 1)]
    all_to_all x1 -> x0, starting transfers between devices: 5.33 us -> none  [shards(): lax.all_to_all(blocks, 'day', split_axis=1, concat_axis=0, tiled=True)[:, 0]]
    unnamed x9 -> x3, local copies, waits for them, and re-layouts: 14.3 us -> 17.5 us
  transfers between devices with their start and end apart: 1 -> 1, of which waited for: 0 -> 0; matrix products, arithmetic and copies ran while one was open for 33% -> 18% of each run, Pallas kernels for 0% -> 0%
where the time goes in v2:
time: 86.7 us; the launch traced here: 86.1 us
  Pallas kernels  63.1 us (73%)
  local copies, waits for them, and re-layouts  21 us (24%)
    pallas_call x1, Pallas kernels, shards(): pl.pallas_call(functools.partial(stack_kernel, lag_count), in_specs=[hbm,...  63.1 us
    unnamed x3, local copies, waits for them, and re-layouts  17.5 us
    reshape x1, local copies, waits for them, and re-layouts, shards(): row_mask = row_mask.reshape(chips, 2 * days * owned, 1)  2.06 us
  transfers between devices with their start and end apart: 1, of which 0 were waited for; matrix products, arithmetic and copies ran while one was open for 18% of the time, Pallas kernels for 0%

profile of v2, /device:TPU:0, one launch (start us, length us, event | category | flops | bytes accessed | tf_op | source)
XLA Modules:
  0.0 86.1 jit_solution(9402800770032558305)
XLA Ops:
  0.6 0.7 convert_element_type.3
  1.3 0.1 reshape.18
  1.5 0.6 collective-permute-start
  2.0 1.4 %copy.14.counts_ref = s32[64,1]{1,0:T(8,128)} copy(s32[64,1]{0,1:T(1,128)} %bitcast.9) | data formatting | bytes 512 | tf_op jit(solution)/shard_map/broadcast_in_dim | solution.py:250
  3.4 13.7 %copy.10 = bf16[4,512,2001]{2,1,0:T(8,128)(2,1)} copy(bf16[4,512,2001]{1,0,2:T(4,128)(2,1)} %param.4) | data formatting | bytes 16392192 | tf_op args[0]
  17.1 0.0 collective-permute-done
  17.1 2.1 %reshape.20.mask_ref = f32[4,512,1]{2,1,0:T(8,128)} reshape(f32[4,8,64]{2,1,0:T(8,128)S(1)} %maximum_bitcast_fusion) | data formatting | bytes 16384 | tf_op jit(solution)/shard_map/reshape | solution.py:219
  19.2 63.1 %stack.1 = (f32[64,2001]{1,0:T(8,128)}, f32[64,2001]{1,0:T(8,128)}) custom-call(bf16[4,8,64,2001]{3,2,1,0:T(8,128)(2,1)} %bitcast.8, f32[4,512,1]{2,1,0:T(8,128)} %reshape.20.mask_ref, s32[64,1]{1,0:T(8,128)} %copy.14.counts_ref, bf16[256,3840]{1,0:T(8,128)(2,1)} %constant.22.clone.strip_hbm), custom_call_target="tpu_custom_call" | custom-call | tf_op jit(solution)/shard_map/stack/pallas_call | solution.py:227
  82.3 1.9 %copy.23 = f32[64,2001]{1,0:T(8,128)} copy(f32[64,2001]{1,0:T(8,128)} %get-tuple-element.8) | data formatting | bytes 1024512
  84.2 1.9 %copy.24 = f32[64,2001]{1,0:T(8,128)} copy(f32[64,2001]{1,0:T(8,128)} %get-tuple-element.9) | data formatting | bytes 1024512
  (3 shorter events, 0.0 us)
Async XLA Ops:
  1.5 15.6 %collective-permute-start = (f32[4,4,64]{2,0,1:T(4,128)S(1)}, f32[4,4,64]{2,0,1:T(4,128)S(1)}, u32[]{:S(2)}, u32[]{:S(2)}) collective-permute-start(f32[4,4,64]{2,0,1:T(4,128)S(1)} %get-tuple-element.3), channel_id=1, source_target_pairs={{0,4},{4,0},{8,12},{12,8},{16,20},{20,16},{24,28},{28,24},{1,5},{5... | collective-permute-start | bytes 12296 | tf_op jit(solution)/shard_map/ppermute | solution.py:217

commit v3 on v2

v3 whole, which is shorter than its diff:
```python
import functools

import jax
import jax.numpy as jnp
import numpy as np
from jax import lax
from jax.experimental import pallas as pl
from jax.experimental.pallas import tpu as pltpu
from jax.sharding import PartitionSpec as P

TILE = 256
MESH = pl.DeviceIdType.MESH
FULL = 32767.0
UNIT = 2.0**20


def padded(lag_count):
    return -(-lag_count // TILE) * TILE


def kernel_strip(lag_count):
    f32 = np.float32
    offset = np.arange(lag_count, dtype=np.int32)
    offset = np.where(offset > lag_count // 2, offset - lag_count, offset)
    angle = f32(np.pi) * offset.astype(f32) / f32(lag_count)
    parity = f32(1) - f32(2) * (offset % 2).astype(f32)
    sine = np.where(offset == 0, f32(1), np.sin(angle)).astype(f32)
    kernel = np.where(offset == 0, f32(0), (np.cos(angle) - parity) / (f32(lag_count) * sine))
    width = padded(lag_count)
    index = np.arange(2 * width - TILE)[None, :] - np.arange(TILE)[:, None] - (width - TILE)
    return kernel.astype(f32)[index % lag_count].astype(jnp.bfloat16)


def codes(values):
    top = jnp.max(jnp.abs(values), axis=1, keepdims=True)
    units = (top * UNIT).astype(jnp.int32) + 1
    step = FULL * UNIT / units.astype(jnp.float32)
    return jnp.round(values * step).astype(jnp.int32), units


def join(high, low):
    return high * 65536 + (low & 65535)


def split(word):
    low = ((word & 65535) ^ 32768) - 32768
    return word >> 16, low


def stack_kernel(
    lag_count, x_hbm, mask_ref, strip_hbm, linear_ref, power_ref,
    rows_ref, stage, strip, table, sums, first_hilbert, mask_in, mask_turned, row_mask, day_weight,
    stat_out, stat_in, words_out, words_in,
    load_sem, stage_sem, strip_sem, swap_send, swap_recv, mask_send, mask_recv,
    stat_send, stat_recv, word_send, word_recv,
):
    width = table.shape[1]
    half = width // 2
    chips, all_days, owned, _ = rows_ref.shape
    days = all_days // 2
    total = all_days * owned
    peers = stat_in.shape[0]
    me, plane = lax.axis_index("day"), lax.axis_index("pair")
    chip, core = me // 2, me % 2
    partner = {"day": me ^ 1, "pair": plane}
    last = width - TILE
    tiles = [slice(j * TILE, min((j + 1) * TILE, lag_count)) for j in range(width // TILE)]

    def mine(g):
        return pltpu.make_async_copy(x_hbm.at[:, 2 * g + core], rows_ref.at[g, pl.ds(0, days)], load_sem.at[g])

    def staged(g):
        return pltpu.make_async_copy(x_hbm.at[:, 2 * g + 1 - core], stage.at[g], stage_sem.at[g])

    def swapped(g):
        return pltpu.make_async_remote_copy(
            stage.at[g], rows_ref.at[g, pl.ds(days, days)], swap_send.at[g], swap_recv.at[g],
            device_id=partner, device_id_type=MESH,
        )

    def peer(o):
        rank = (2 * plane + core + o) % (peers + 1)
        return {"day": 2 * chip + rank % 2, "pair": rank // 2}

    def told(o):
        return pltpu.make_async_remote_copy(
            stat_out, stat_in.at[o - 1], stat_send.at[o - 1], stat_recv.at[o - 1],
            device_id=peer(o), device_id_type=MESH,
        )

    def owner(o):
        return {"day": 2 * (chip ^ o) + core, "pair": plane}

    def shipped(o):
        return pltpu.make_async_remote_copy(
            words_out.at[o - 1], words_in.at[o - 1], word_send.at[o - 1], word_recv.at[o - 1],
            device_id=owner(o), device_id_type=MESH,
        )

    order = [chip ^ o for o in range(chips - 1, -1, -1)]
    for g in order:
        staged(g).start()
        mine(g).start()
    strip_copy = pltpu.make_async_copy(strip_hbm, strip, strip_sem)
    strip_copy.start()

    barrier = pltpu.get_barrier_semaphore()
    for o in range(1, peers + 1):
        pl.semaphore_signal(barrier, inc=1, device_id=peer(o), device_id_type=MESH)
    for o in range(1, chips):
        pl.semaphore_signal(barrier, inc=1, device_id=owner(o), device_id_type=MESH)
    pl.semaphore_wait(barrier, peers + chips - 1)

    mask_copy = pltpu.make_async_remote_copy(
        mask_ref, mask_in, mask_send, mask_recv, device_id=partner, device_id_type=MESH
    )
    mask_copy.start()
    for g in order:
        staged(g).wait()
        swapped(g).start()
    mask_copy.wait_recv()
    both_masks = jnp.concatenate([mask_ref[...], mask_in[...]], axis=0).astype(jnp.float32)
    mask_turned[...] = both_masks.T

    def mask_rows(block, count):
        rows = mask_turned[pl.ds(pl.multiple_of(block * owned, owned), owned), :]
        return jnp.concatenate([rows[:, d : d + 1] for d in range(count)], axis=0)

    def statistics(step, carry):
        g = chip ^ (chips - 1 - step)
        mine(g).wait()
        row_mask[g] = mask_rows(2 * g + core, all_days)
        for x_ref, rows in ((rows_ref.at[g, pl.ds(0, days)], row_mask[g, : days * owned]),
                            (stage.at[g], mask_rows(2 * g + 1 - core, days))):
            x = x_ref[...].reshape(days * owned, lag_count).astype(jnp.float32)
            energy = jnp.sum(x * x, axis=1, keepdims=True) * rows
            both = jnp.concatenate(
                [jnp.broadcast_to(energy, (days * owned, 128)), jnp.broadcast_to(rows, (days * owned, 128))], axis=1
            )
            carry = carry + jnp.sum(both.reshape(days, owned, 256), axis=1)
        return carry

    found = lax.fori_loop(0, chips, statistics, jnp.zeros((days, 256), jnp.float32))
    none = jnp.zeros_like(found)
    stat_out[...] = jnp.where(
        core == 0, jnp.concatenate([found, none], axis=0), jnp.concatenate([none, found], axis=0)
    )
    for o in range(1, peers + 1):
        told(o).start()

    strip_copy.wait()
    for i in range(width // TILE):
        start = width - TILE - i * TILE
        table[pl.ds(i * TILE, TILE), :] = strip[:, start : start + width]
    sums[:, :, last:] = jnp.zeros((3, owned, TILE), jnp.float32)

    def transform(g, cols):
        lhs = rows_ref[g].reshape(total, lag_count)
        return jnp.dot(lhs, table[:lag_count, cols], preferred_element_type=jnp.float32)

    def add_days(g, scale, cols, hilbert):
        size = cols.stop - cols.start
        real = scale * rows_ref[g, :, :, cols].reshape(total, size).astype(jnp.float32)
        imag = scale * hilbert
        inverse = lax.rsqrt(real * real + imag * imag + 0.25)
        for k, term in enumerate((real, real * inverse, imag * inverse)):
            sums[k, :, cols] = jnp.sum(term.reshape(all_days, owned, size), axis=0)

    def encode(o):
        linear, linear_units = codes(sums[0])
        first, first_units = codes(sums[1])
        second, second_units = codes(sums[2])
        words_out[o - 1, :, :width] = join(first, second)
        words_out[o - 1, :, width : width + half] = join(linear[:, :half], linear[:, half:])
        pick = lax.broadcasted_iota(jnp.int32, (owned, 128), 1)
        words_out[o - 1, :, width + half :] = jnp.where(
            pick == 0, linear_units, jnp.where(pick == 1, first_units, second_units)
        )
        shipped(o).start()

    swapped(order[0]).wait_recv()
    for cols in tiles:
        first_hilbert[:, cols] = transform(order[0], cols)

    for o in range(1, peers + 1):
        told(o).wait_recv()
    stats = stat_out[...]
    for o in range(peers):
        stats = stats + stat_in[o]
    weight = lax.rsqrt(stats[:, :128] / (lag_count * jnp.maximum(stats[:, 128:], 1.0)) + 0.1)
    weight = jnp.where(core == 0, weight, jnp.concatenate([weight[days:], weight[:days]], axis=0))
    for d in range(all_days):
        day_weight[pl.ds(d * owned, owned), :] = jnp.broadcast_to(weight[d : d + 1, :1], (owned, 1))

    scale = day_weight[...] * row_mask[order[0]]
    for cols in tiles:
        add_days(order[0], scale, cols, first_hilbert[:, cols])
    encode(chips - 1)

    def block(step, carry):
        o = chips - 1 - step
        g = chip ^ o
        swapped(g).wait_recv()
        scale = day_weight[...] * row_mask[g]
        for cols in tiles:
            add_days(g, scale, cols, transform(g, cols))

        @pl.when(o > 0)
        def _():
            encode(o)

        return carry

    lax.fori_loop(1, chips, block, 0)

    def arrive(step, carry):
        o = chips - 1 - step
        shipped(o).wait_recv()
        units = words_in[o - 1, :, width + half :].astype(jnp.float32) * (1.0 / (FULL * UNIT))
        left, right = split(words_in[o - 1, :, width : width + half])
        sums[0, :, :half] += left.astype(jnp.float32) * units[:, 0:1]
        sums[0, :, half:] += right.astype(jnp.float32) * units[:, 0:1]
        first, second = split(words_in[o - 1, :, :width])
        sums[1] += first.astype(jnp.float32) * units[:, 1:2]
        sums[2] += second.astype(jnp.float32) * units[:, 2:3]
        return carry

    lax.fori_loop(0, chips - 1, arrive, 0)
    real, imag = sums[1, :, :lag_count], sums[2, :, :lag_count]
    linear_ref[...] = sums[0, :, :lag_count]
    power_ref[...] = real * real + imag * imag

    mask_copy.wait_send()
    for g in range(chips):
        swapped(g).wait_send()
    for o in range(1, peers + 1):
        told(o).wait_send()
    for o in range(1, chips):
        shipped(o).wait_send()


def shards(correlations, mask, counts):
    days, pairs, lag_count = correlations.shape
    groups = lax.axis_size("day")
    chips = groups // 2
    owned = pairs // groups
    width = padded(lag_count)
    peers = 2 * lax.axis_size("pair") - 1

    strip = jnp.asarray(kernel_strip(lag_count))
    size = width + width // 2 + 128
    out = jax.ShapeDtypeStruct((owned, lag_count), jnp.float32)
    vmem = pl.BlockSpec(memory_space=pltpu.VMEM)
    hbm = pl.BlockSpec(memory_space=pl.ANY)
    dma = pltpu.SemaphoreType.DMA
    linear_sum, power = pl.pallas_call(
        functools.partial(stack_kernel, lag_count),
        in_specs=[hbm, vmem, hbm],
        out_specs=(vmem, vmem),
        out_shape=(out, out),
        scratch_shapes=[
            pltpu.VMEM((chips, 2 * days, owned, lag_count), jnp.bfloat16),
            pltpu.VMEM((chips, days, owned, lag_count), jnp.bfloat16),
            pltpu.VMEM(strip.shape, jnp.bfloat16),
            pltpu.VMEM((width, width), jnp.bfloat16),
            pltpu.VMEM((3, owned, width), jnp.float32),
            pltpu.VMEM((2 * days * owned, width), jnp.float32),
            pltpu.VMEM((days, pairs), jnp.int32),
            pltpu.VMEM((pairs, 2 * days), jnp.float32),
            pltpu.VMEM((chips, 2 * days * owned, 1), jnp.float32),
            pltpu.VMEM((2 * days * owned, 1), jnp.float32),
            pltpu.VMEM((2 * days, 256), jnp.float32),
            pltpu.VMEM((peers, 2 * days, 256), jnp.float32),
            pltpu.VMEM((chips - 1, owned, size), jnp.int32),
            pltpu.VMEM((chips - 1, owned, size), jnp.int32),
            dma((chips,)), dma((chips,)), dma, dma((chips,)), dma((chips,)), dma, dma,
            dma((peers,)), dma((peers,)), dma((chips - 1,)), dma((chips - 1,)),
        ],
        compiler_params=pltpu.CompilerParams(
            vmem_limit_bytes=62 * 2**20, collective_id=0, has_side_effects=True
        ),
        name="stack",
    )(correlations.reshape(days, groups, owned, lag_count), mask, strip)
    divisor = jnp.maximum(counts.astype(jnp.float32), 1.0)[:, None]
    linear = linear_sum / divisor
    return (linear * (power / (divisor * divisor)), linear)


def solution(mesh):
    placed = (P("day", "pair", None), P("day", "pair"), P(("pair", "day")))
    return jax.shard_map(
        shards,
        mesh=mesh,
        in_specs=placed,
        out_specs=(P(("pair", "day"), None), P(("pair", "day"), None)),
        check_vma=False,
    )
```

time: 86.7 us -> 74.9 us (0.86)
  local copies, waits for them, and re-layouts: 21 us -> 13.7 us
  Pallas kernels: 63.1 us -> 57.7 us
  other arithmetic: 0.72 us -> 2.34 us
    pallas_call x1, Pallas kernels: 63.1 us -> 57.7 us  [shards(): pl.pallas_call(functools.partial(stack_kernel, lag_count), in_specs=[hbm,...]
    unnamed x3, local copies, waits for them, and re-layouts: 17.5 us -> 13.7 us
    mul x0 -> x1, other arithmetic: none -> 2.33 us  [shards(): return (linear * (power / (divisor * divisor)), linear)]
    reshape x2 -> x0, local copies, waits for them, and re-layouts: 2.15 us -> none  [the longest x1 2.06 us: shards(): row_mask = row_mask.reshape(chips, 2 * days * owned, 1)]
    broadcast_in_dim x1 -> x0, local copies, waits for them, and re-layouts: 1.36 us -> none  [shards(): counts[:, None]]
  transfers between devices with their start and end apart: 1 -> 0, of which waited for: 0 -> 0; matrix products, arithmetic and copies ran while one was open for 18% -> 0% of each run, Pallas kernels for 0% -> 0%
where the time goes in v3:
time: 74.9 us; the launch traced here: 74.4 us
  Pallas kernels  57.7 us (77%)
  local copies, waits for them, and re-layouts  13.7 us (18%)
  other arithmetic  2.34 us (3%)
    pallas_call x1, Pallas kernels, shards(): pl.pallas_call(functools.partial(stack_kernel, lag_count), in_specs=[hbm,...  57.7 us
    unnamed x3, local copies, waits for them, and re-layouts  13.7 us
    mul x1, other arithmetic, shards(): return (linear * (power / (divisor * divisor)), linear)  2.33 us

profile of v3, /device:TPU:0, one launch (start us, length us, event | category | flops | bytes accessed | tf_op | source)
XLA Modules:
  0.0 74.4 jit_solution(992782759805313903)
XLA Ops:
  0.6 13.7 %copy.6 = bf16[4,512,2001]{2,1,0:T(8,128)(2,1)} copy(bf16[4,512,2001]{1,0,2:T(4,128)(2,1)} %param.4) | data formatting | bytes 16392192 | tf_op args[0]
  14.3 0.0 copy-start
  14.3 57.7 %stack.1 = (f32[64,2001]{1,0:T(8,128)}, f32[64,2001]{1,0:T(8,128)}) custom-call(bf16[4,8,64,2001]{3,2,1,0:T(8,128)(2,1)} %bitcast.1, s32[4,512]{1,0:T(4,128)} %mask_ref.1, bf16[256,3840]{1,0:T(8,128)(2,1)} %constant.4.clone.strip_hbm), custom_call_target="tpu_custom_call" | custom-call | tf_op jit(solution)/shard_map/stack/pallas_call | solution.py:256
  72.1 0.0 copy-done
  72.1 2.3 %divide_multiply_fusion = (f32[64,2001]{1,0:T(8,128)}, f32[64,2001]{1,0:T(8,128)}) fusion(f32[64,2001]{1,0:T(8,128)} %get-tuple-element.5, f32[64]{0:T(128)S(1)} %get-tuple-element.9, f32[64,2001]{1,0:T(8,128)} %get-tuple-element.4, f32[64]{0:T(128)S(1)} %get-tuple-element.8), kind=kLoop, calls=%fused_computation | loop fusion | flops 384192 | bytes 2049536 | tf_op jit(solution)/shard_map/mul | solution.py:286
  (1 shorter events, 0.0 us)
Async XLA Ops:
  14.3 57.7 %copy-start = (s32[64]{0:T(128)S(1)}, s32[64]{0:T(128)}, u32[]{:S(2)}) copy-start(s32[64]{0:T(128)} %param.6) | copy-start | bytes 772

commit v4 on v3

--- a/solution.py
+++ b/solution.py
@@ -59,6 +59,8 @@
     chips, all_days, owned, _ = rows_ref.shape
     days = all_days // 2
     total = all_days * owned
+    part = owned // 2
+    pieces = words_out.shape[0]
     peers = stat_in.shape[0]
     me, plane = lax.axis_index("day"), lax.axis_index("pair")
     chip, core = me // 2, me % 2
@@ -91,13 +93,14 @@
     def owner(o):
         return {"day": 2 * (chip ^ o) + core, "pair": plane}
 
-    def shipped(o):
+    def shipped(piece, o):
         return pltpu.make_async_remote_copy(
-            words_out.at[o - 1], words_in.at[o - 1], word_send.at[o - 1], word_recv.at[o - 1],
+            words_out.at[piece], words_in.at[piece], word_send.at[piece], word_recv.at[piece],
             device_id=owner(o), device_id_type=MESH,
         )
 
-    order = [chip ^ o for o in range(chips - 1, -1, -1)]
+    far = range(chips - 1, 3, -1)
+    order = [chip ^ o for o in (3, *far, 1, 2, 0)]
     for g in order:
         staged(g).start()
         mine(g).start()
@@ -129,8 +132,9 @@
     def statistics(step, carry):
         g = chip ^ (chips - 1 - step)
         mine(g).wait()
-        row_mask[g] = mask_rows(2 * g + core, all_days)
-        for x_ref, rows in ((rows_ref.at[g, pl.ds(0, days)], row_mask[g, : days * owned]),
+        of_pairs = mask_rows(2 * g + core, all_days)
+        row_mask[g] = of_pairs.reshape(all_days, owned, 1)
+        for x_ref, rows in ((rows_ref.at[g, pl.ds(0, days)], of_pairs[: days * owned]),
                             (stage.at[g], mask_rows(2 * g + 1 - core, days))):
             x = x_ref[...].reshape(days * owned, lag_count).astype(jnp.float32)
             energy = jnp.sum(x * x, axis=1, keepdims=True) * rows
@@ -154,33 +158,46 @@
         table[pl.ds(i * TILE, TILE), :] = strip[:, start : start + width]
     sums[:, :, last:] = jnp.zeros((3, owned, TILE), jnp.float32)
 
-    def transform(g, cols):
-        lhs = rows_ref[g].reshape(total, lag_count)
+    def transform(g, here, cols):
+        lhs = rows_ref[g, :, here, :].reshape(-1, lag_count)
         return jnp.dot(lhs, table[:lag_count, cols], preferred_element_type=jnp.float32)
 
-    def add_days(g, scale, cols, hilbert):
+    def add_days(g, here, cols, hilbert):
         size = cols.stop - cols.start
-        real = scale * rows_ref[g, :, :, cols].reshape(total, size).astype(jnp.float32)
+        count = hilbert.shape[0] // all_days
+        scale = (day_weight[:, :count] * row_mask[g, :, here, :]).reshape(-1, 1)
+        real = scale * rows_ref[g, :, here, cols].reshape(-1, size).astype(jnp.float32)
         imag = scale * hilbert
         inverse = lax.rsqrt(real * real + imag * imag + 0.25)
         for k, term in enumerate((real, real * inverse, imag * inverse)):
-            sums[k, :, cols] = jnp.sum(term.reshape(all_days, owned, size), axis=0)
-
-    def encode(o):
-        linear, linear_units = codes(sums[0])
-        first, first_units = codes(sums[1])
-        second, second_units = codes(sums[2])
-        words_out[o - 1, :, :width] = join(first, second)
-        words_out[o - 1, :, width : width + half] = join(linear[:, :half], linear[:, half:])
-        pick = lax.broadcasted_iota(jnp.int32, (owned, 128), 1)
-        words_out[o - 1, :, width + half :] = jnp.where(
+            sums[k, :count, cols] = jnp.sum(term.reshape(all_days, count, size), axis=0)
+
+    def encode(piece, rows, o):
+        linear, linear_units = codes(sums[0, rows])
+        first, first_units = codes(sums[1, rows])
+        second, second_units = codes(sums[2, rows])
+        words_out[piece, :, :width] = join(first, second)
+        words_out[piece, :, width : width + half] = join(linear[:, :half], linear[:, half:])
+        pick = lax.broadcasted_iota(jnp.int32, (part, 128), 1)
+        words_out[piece, :, width + half :] = jnp.where(
             pick == 0, linear_units, jnp.where(pick == 1, first_units, second_units)
         )
-        shipped(o).start()
+        shipped(piece, o).start()
+
+    def decode(piece, rows):
+        units = words_in[piece, :, width + half :].astype(jnp.float32) * (1.0 / (FULL * UNIT))
+        left, right = split(words_in[piece, :, width : width + half])
+        sums[0, rows, :half] += left.astype(jnp.float32) * units[:, 0:1]
+        sums[0, rows, half:] += right.astype(jnp.float32) * units[:, 0:1]
+        first, second = split(words_in[piece, :, :width])
+        sums[1, rows] += first.astype(jnp.float32) * units[:, 1:2]
+        sums[2, rows] += second.astype(jnp.float32) * units[:, 2:3]
+
+    whole, low, high = pl.ds(0, owned), pl.ds(0, part), pl.ds(part, part)
 
     swapped(order[0]).wait_recv()
     for cols in tiles:
-        first_hilbert[:, cols] = transform(order[0], cols)
+        first_hilbert[:, cols] = transform(order[0], whole, cols)
 
     for o in range(1, peers + 1):
         told(o).wait_recv()
@@ -190,42 +207,57 @@
     weight = lax.rsqrt(stats[:, :128] / (lag_count * jnp.maximum(stats[:, 128:], 1.0)) + 0.1)
     weight = jnp.where(core == 0, weight, jnp.concatenate([weight[days:], weight[:days]], axis=0))
     for d in range(all_days):
-        day_weight[pl.ds(d * owned, owned), :] = jnp.broadcast_to(weight[d : d + 1, :1], (owned, 1))
-
-    scale = day_weight[...] * row_mask[order[0]]
+        day_weight[d] = jnp.broadcast_to(weight[d : d + 1, :1], (owned, 1))
+
     for cols in tiles:
-        add_days(order[0], scale, cols, first_hilbert[:, cols])
-    encode(chips - 1)
-
-    def block(step, carry):
+        add_days(order[0], whole, cols, first_hilbert[:, cols])
+    encode(0, low, 1)
+    encode(1, high, 2)
+
+    def far_block(step, carry):
         o = chips - 1 - step
+        swapped(chip ^ o).wait_recv()
+        for cols in tiles:
+            add_days(chip ^ o, whole, cols, transform(chip ^ o, whole, cols))
+        encode(2 * o - 2, low, o)
+        encode(2 * o - 1, high, o)
+        return carry
+
+    if chips > 4:
+        lax.fori_loop(0, chips - 4, far_block, 0)
+
+    def near_half(q, carry):
+        o = 1 + q % 2
         g = chip ^ o
-        swapped(g).wait_recv()
-        scale = day_weight[...] * row_mask[g]
+        here = pl.ds(pl.multiple_of(((q + q // 2) % 2) * part, part), part)
+
+        @pl.when(q < 2)
+        def _():
+            swapped(g).wait_recv()
+
         for cols in tiles:
-            add_days(g, scale, cols, transform(g, cols))
-
-        @pl.when(o > 0)
+            add_days(g, here, cols, transform(g, here, cols))
+
+        @pl.when(q >= 2)
         def _():
-            encode(o)
-
+            shipped(3 - q, o).wait_recv()
+            decode(3 - q, low)
+
+        encode(2 + q, low, o)
         return carry
 
-    lax.fori_loop(1, chips, block, 0)
-
-    def arrive(step, carry):
-        o = chips - 1 - step
-        shipped(o).wait_recv()
-        units = words_in[o - 1, :, width + half :].astype(jnp.float32) * (1.0 / (FULL * UNIT))
-        left, right = split(words_in[o - 1, :, width : width + half])
-        sums[0, :, :half] += left.astype(jnp.float32) * units[:, 0:1]
-        sums[0, :, half:] += right.astype(jnp.float32) * units[:, 0:1]
-        first, second = split(words_in[o - 1, :, :width])
-        sums[1] += first.astype(jnp.float32) * units[:, 1:2]
-        sums[2] += second.astype(jnp.float32) * units[:, 2:3]
+    lax.fori_loop(0, 4, near_half, 0)
+    swapped(chip).wait_recv()
+    for cols in tiles:
+        add_days(chip, whole, cols, transform(chip, whole, cols))
+
+    def arrive(piece, carry):
+        turn = piece + jnp.where(piece // 2 == 2, 1, 0)
+        shipped(piece, 1).wait_recv()
+        decode(piece, pl.ds(pl.multiple_of((turn % 2) * part, part), part))
         return carry
 
-    lax.fori_loop(0, chips - 1, arrive, 0)
+    lax.fori_loop(2, pieces, arrive, 0)
     real, imag = sums[1, :, :lag_count], sums[2, :, :lag_count]
     linear_ref[...] = sums[0, :, :lag_count]
     power_ref[...] = real * real + imag * imag
@@ -235,8 +267,8 @@
         swapped(g).wait_send()
     for o in range(1, peers + 1):
         told(o).wait_send()
-    for o in range(1, chips):
-        shipped(o).wait_send()
+    for piece in range(pieces):
+        shipped(piece, 1).wait_send()
 
 
 def shards(correlations, mask, counts):
@@ -249,6 +281,7 @@
 
     strip = jnp.asarray(kernel_strip(lag_count))
     size = width + width // 2 + 128
+    pieces = 2 * chips - 2
     out = jax.ShapeDtypeStruct((owned, lag_count), jnp.float32)
     vmem = pl.BlockSpec(memory_space=pltpu.VMEM)
     hbm = pl.BlockSpec(memory_space=pl.ANY)
@@ -267,14 +300,14 @@
             pltpu.VMEM((2 * days * owned, width), jnp.float32),
             pltpu.VMEM((days, pairs), jnp.int32),
             pltpu.VMEM((pairs, 2 * days), jnp.float32),
-            pltpu.VMEM((chips, 2 * days * owned, 1), jnp.float32),
-            pltpu.VMEM((2 * days * owned, 1), jnp.float32),
+            pltpu.VMEM((chips, 2 * days, owned, 1), jnp.float32),
+            pltpu.VMEM((2 * days, owned, 1), jnp.float32),
             pltpu.VMEM((2 * days, 256), jnp.float32),
             pltpu.VMEM((peers, 2 * days, 256), jnp.float32),
-            pltpu.VMEM((chips - 1, owned, size), jnp.int32),
-            pltpu.VMEM((chips - 1, owned, size), jnp.int32),
+            pltpu.VMEM((pieces, owned // 2, size), jnp.int32),
+            pltpu.VMEM((pieces, owned // 2, size), jnp.int32),
             dma((chips,)), dma((chips,)), dma, dma((chips,)), dma((chips,)), dma, dma,
-            dma((peers,)), dma((peers,)), dma((chips - 1,)), dma((chips - 1,)),
+            dma((peers,)), dma((peers,)), dma((pieces,)), dma((pieces,)),
         ],
         compiler_params=pltpu.CompilerParams(
             vmem_limit_bytes=62 * 2**20, collective_id=0, has_side_effects=True

time: 74.9 us -> 64.8 us (0.87)
  Pallas kernels: 57.7 us -> 47.6 us
    pallas_call x1, Pallas kernels: 57.7 us -> 47.6 us  [shards(): pl.pallas_call(functools.partial(stack_kernel, lag_count), in_specs=[hbm,...]
where the time goes in v4:
time: 64.8 us; the launch traced here: 64.3 us
  Pallas kernels  47.6 us (73%)
  local copies, waits for them, and re-layouts  13.7 us (21%)
  other arithmetic  2.34 us (4%)
  between operations  0.65 us (1%)
    pallas_call x1, Pallas kernels, shards(): pl.pallas_call(functools.partial(stack_kernel, lag_count), in_specs=[hbm,...  47.6 us
    unnamed x3, local copies, waits for them, and re-layouts  13.7 us
    mul x1, other arithmetic, shards(): return (linear * (power / (divisor * divisor)), linear)  2.33 us

profile of v4, /device:TPU:0, one launch (start us, length us, event | category | flops | bytes accessed | tf_op | source)
XLA Modules:
  0.0 64.3 jit_solution(10081690417154633692)
XLA Ops:
  0.6 13.7 %copy.6 = bf16[4,512,2001]{2,1,0:T(8,128)(2,1)} copy(bf16[4,512,2001]{1,0,2:T(4,128)(2,1)} %param.4) | data formatting | bytes 16392192 | tf_op args[0]
  14.3 0.0 copy-start
  14.3 47.6 %stack.1 = (f32[64,2001]{1,0:T(8,128)}, f32[64,2001]{1,0:T(8,128)}) custom-call(bf16[4,8,64,2001]{3,2,1,0:T(8,128)(2,1)} %bitcast.1, s32[4,512]{1,0:T(4,128)} %mask_ref.1, bf16[256,3840]{1,0:T(8,128)(2,1)} %constant.4.clone.strip_hbm), custom_call_target="tpu_custom_call" | custom-call | tf_op jit(solution)/shard_map/stack/pallas_call | solution.py:289
  62.0 0.0 copy-done
  62.0 2.3 %divide_multiply_fusion = (f32[64,2001]{1,0:T(8,128)}, f32[64,2001]{1,0:T(8,128)}) fusion(f32[64,2001]{1,0:T(8,128)} %get-tuple-element.5, f32[64]{0:T(128)S(1)} %get-tuple-element.9, f32[64,2001]{1,0:T(8,128)} %get-tuple-element.4, f32[64]{0:T(128)S(1)} %get-tuple-element.8), kind=kLoop, calls=%fused_computation | loop fusion | flops 384192 | bytes 2049536 | tf_op jit(solution)/shard_map/mul | solution.py:319
  (1 shorter events, 0.0 us)
Async XLA Ops:
  14.3 47.6 %copy-start = (s32[64]{0:T(128)S(1)}, s32[64]{0:T(128)}, u32[]{:S(2)}) copy-start(s32[64]{0:T(128)} %param.6) | copy-start | bytes 772

commit v5 on v4

--- a/solution.py
+++ b/solution.py
@@ -101,17 +101,22 @@
 
     far = range(chips - 1, 3, -1)
     order = [chip ^ o for o in (3, *far, 1, 2, 0)]
+    strip_copy = pltpu.make_async_copy(strip_hbm, strip, strip_sem)
+    strip_copy.start()
     for g in order:
         staged(g).start()
         mine(g).start()
-    strip_copy = pltpu.make_async_copy(strip_hbm, strip, strip_sem)
-    strip_copy.start()
 
     barrier = pltpu.get_barrier_semaphore()
     for o in range(1, peers + 1):
         pl.semaphore_signal(barrier, inc=1, device_id=peer(o), device_id_type=MESH)
     for o in range(1, chips):
         pl.semaphore_signal(barrier, inc=1, device_id=owner(o), device_id_type=MESH)
+    strip_copy.wait()
+    for i in range(width // TILE):
+        start = width - TILE - i * TILE
+        table[pl.ds(i * TILE, TILE), :] = strip[:, start : start + width]
+    sums[:, :, last:] = jnp.zeros((3, owned, TILE), jnp.float32)
     pl.semaphore_wait(barrier, peers + chips - 1)
 
     mask_copy = pltpu.make_async_remote_copy(
@@ -151,12 +156,6 @@
     )
     for o in range(1, peers + 1):
         told(o).start()
-
-    strip_copy.wait()
-    for i in range(width // TILE):
-        start = width - TILE - i * TILE
-        table[pl.ds(i * TILE, TILE), :] = strip[:, start : start + width]
-    sums[:, :, last:] = jnp.zeros((3, owned, TILE), jnp.float32)
 
     def transform(g, here, cols):
         lhs = rows_ref[g, :, here, :].reshape(-1, lag_count)
@@ -310,13 +309,13 @@
             dma((peers,)), dma((peers,)), dma((pieces,)), dma((pieces,)),
         ],
         compiler_params=pltpu.CompilerParams(
-            vmem_limit_bytes=62 * 2**20, collective_id=0, has_side_effects=True
+            vmem_limit_bytes=46 * 2**20, collective_id=0, has_side_effects=True
         ),
         name="stack",
     )(correlations.reshape(days, groups, owned, lag_count), mask, strip)
-    divisor = jnp.maximum(counts.astype(jnp.float32), 1.0)[:, None]
-    linear = linear_sum / divisor
-    return (linear * (power / (divisor * divisor)), linear)
+    inverse = (1.0 / jnp.maximum(counts.astype(jnp.float32), 1.0))[:, None]
+    linear = linear_sum * inverse
+    return (linear * (power * (inverse * inverse)), linear)
 
 
 def solution(mesh):

time: 64.8 us -> 61.8 us (0.954)
  Pallas kernels: 47.6 us -> 45.7 us
  other arithmetic: 2.34 us -> 1.11 us
    pallas_call x1, Pallas kernels: 47.6 us -> 45.7 us  [shards(): pl.pallas_call(functools.partial(stack_kernel, lag_count), in_specs=[hbm,...]
    mul x1 -> x2, other arithmetic: 2.33 us -> 1.11 us  [shards(): return (linear * (power * (inverse * inverse)), linear)]
    unnamed x3 -> x7, local copies, waits for them, and re-layouts: 13.7 us -> 13.9 us
where the time goes in v5:
time: 61.8 us; the launch traced here: 61.4 us
  Pallas kernels  45.7 us (74%)
  local copies, waits for them, and re-layouts  13.9 us (22%)
  other arithmetic  1.11 us (2%)
  between operations  0.67 us (1%)
    pallas_call x1, Pallas kernels, shards(): pl.pallas_call(functools.partial(stack_kernel, lag_count), in_specs=[hbm,...  45.7 us
    unnamed x7, local copies, waits for them, and re-layouts  13.9 us

profile of v5, /device:TPU:0, one launch (start us, length us, event | category | flops | bytes accessed | tf_op | source)
XLA Modules:
  0.0 61.4 jit_solution(11408501458923064006)
XLA Ops:
  0.6 0.0 copy-start
  0.6 0.0 copy-start.1
  0.7 13.8 %copy.6 = bf16[4,512,2001]{2,1,0:T(8,128)(2,1)} copy(bf16[4,512,2001]{1,0,2:T(4,128)(2,1)} %param.4) | data formatting | bytes 16392192 | tf_op args[0]
  14.5 0.0 copy-start.2
  14.5 0.0 copy-done
  14.5 0.0 copy-done.1
  14.5 45.7 %stack.1 = (f32[64,2001]{1,0:T(8,128)S(1)}, f32[64,2001]{1,0:T(8,128)S(1)}) custom-call(bf16[4,8,64,2001]{3,2,1,0:T(8,128)(2,1)} %bitcast.1, s32[4,512]{1,0:T(4,128)S(1)} %copy-done.1, bf16[256,3840]{1,0:T(8,128)(2,1)S(1)} %copy-done), custom_call_target="tpu_custom_call" | custom-call | tf_op jit(solution)/shard_map/stack/pallas_call | solution.py:288
  60.2 0.0 copy-done.2
  60.2 1.1 %multiply_multiply_fusion = (f32[64,2001]{1,0:T(8,128)}, f32[64,2001]{1,0:T(8,128)}) fusion(f32[64,2001]{1,0:T(8,128)S(1)} %get-tuple-element.5, f32[64]{0:T(128)S(1)} %get-tuple-element.8, f32[64,2001]{1,0:T(8,128)S(1)} %get-tuple-element.4, f32[64]{0:T(128)S(1)} %get-tuple-element.9), kind=kLoop, calls=%fused_computation | loop fusion | flops 384192 | bytes 2049536 | tf_op jit(solution)/shard_map/mul | solution.py:318
  (1 shorter events, 0.0 us)
Async XLA Ops:
  0.6 13.9 %copy-start = (bf16[256,3840]{1,0:T(8,128)(2,1)S(1)}, bf16[256,3840]{1,0:T(8,128)(2,1)}, u32[]{:S(2)}) copy-start(bf16[256,3840]{1,0:T(8,128)(2,1)} %constant.4.clone.strip_hbm) | copy-start | bytes 5898244
  0.6 13.9 %copy-start.1 = (s32[4,512]{1,0:T(4,128)S(1)}, s32[4,512]{1,0:T(4,128)}, u32[]{:S(2)}) copy-start(s32[4,512]{1,0:T(4,128)} %mask_ref.1) | copy-start | bytes 24580
  14.5 45.7 %copy-start.2 = (s32[64]{0:T(128)S(1)}, s32[64]{0:T(128)}, u32[]{:S(2)}) copy-start(s32[64]{0:T(128)} %param.6) | copy-start | bytes 772
